TPU v7x, 32 devices: a whole 2x2x4 slice. The times are simulated.
32 devices in a mesh: map: 8 (over z, y), rep: 4 (over x, core).
Axes of the slice: x: 2, y: 2, z: 4, core: 2. Of those that a mesh axis runs over, the one named last changes fastest.
Arguments:
- field_bricks: bfloat16 [16384, 512], P('map'), may hold values from -6 to 6
- owners: int32 [2048, 64], P('map', 'rep'), may hold values from 0 to 7, as said below
- bricks: int32 [2048, 64], P('map', 'rep'), may hold values from 0 to 2047
- corners: int32 [2048, 64], P('map', 'rep'), may hold values from 0 to 342
- fraction: float32 [3, 2048, 64], P(None, 'map', 'rep'), may hold values from 0 to 1
Outputs:
- trajectory_cost: float32 [2048], P('map')
- waypoint_grad: float32 [3, 2048, 64], P(None, 'map', 'rep')
Inputs may be any that keep to these rules, and one draw needn't show every extreme that they name: `owners`: among one device's 4096 waypoints at most 2048 have the same owner, and in every draw some owner has exactly 2048 of them.
All inputs are finite; a program needn't handle non-finite values.
Results may differ from a plain program's by a relative error of at most 0.0003.
Values sent between devices are 32-bit elements; how exact they have to be, the bound alone decides.
A program may use at most 64 MiB of HBM per device.

v0:
```python
import functools

import jax
import jax.numpy as jnp
from jax import lax
from jax.experimental import pallas as pl
from jax.experimental.pallas import tpu as pltpu
from jax.sharding import PartitionSpec as P

margin = 0.5
LANES = 128
VMEM = pltpu.VMEM
SMEM = pltpu.SMEM


MESH = pl.DeviceIdType.MESH


def lanes_of(x):
    return jnp.concatenate(
        [x[:, h * LANES : (h + 1) * LANES] for h in range(x.shape[1] // LANES)], axis=0
    )


def iota(shape, axis):
    return lax.broadcasted_iota(jnp.int32, shape, axis)


def each(count, body, unrolled):
    if count <= unrolled:
        for i in range(count):
            body(i)
    else:
        lax.fori_loop(0, count, lambda i, z: (body(i), z)[1], 0)


def dispatch_kernel(
    devices, tiles, owners_ref, bricks_ref, corners_ref, frac_ref,
    out_ref, own_ref, rank_ref, meta_ref,
    data_ref, pos_ref, meta_s, sem,
):
    own = lanes_of(owners_ref[...])
    chunks = own.shape[0]
    bricks = bricks_ref[...]
    corners = corners_ref[...]
    cx = (corners * 1338) >> 16
    cxy = (corners * 9363) >> 16
    code = bricks * 512 + cx * 64 + (cxy - cx * 7) * 8 + (corners - cxy * 7)
    code = lanes_of(code.astype(jnp.float32))
    for k in range(2):
        data_ref[:, 4 * k, :] = code
    for f in range(3):
        part = lanes_of(frac_ref[f])
        for k in range(2):
            data_ref[:, 4 * k + 1 + f, :] = part
    own_ref[...] = own
    out_ref[...] = jnp.zeros_like(out_ref)

    upper = (iota((LANES, LANES), 0) <= iota((LANES, LANES), 1)).astype(jnp.float32).astype(jnp.bfloat16)
    ones = jnp.ones((LANES, LANES), jnp.bfloat16)
    before = (iota((chunks, chunks), 0) > iota((chunks, chunks), 1)).astype(jnp.float32).astype(jnp.bfloat16)
    lane = iota((chunks, LANES), 1)
    rank = jnp.zeros((chunks, LANES), jnp.float32)
    pos = jnp.zeros((chunks, LANES), jnp.float32)
    start = jnp.zeros((chunks, LANES), jnp.float32)
    meta = jnp.zeros((chunks, LANES), jnp.int32)
    for o in range(devices):
        member = own == o
        m16 = member.astype(jnp.float32).astype(jnp.bfloat16)
        incl = jnp.dot(m16, upper, preferred_element_type=jnp.float32) - 1.0
        total = jnp.dot(m16, ones, preferred_element_type=jnp.float32)
        off = jnp.dot(before, total.astype(jnp.bfloat16), preferred_element_type=jnp.float32)
        rank = jnp.where(member, incl + off, rank)
        pos = jnp.where(member, incl + start, pos)
        meta = jnp.where(lane == o, off.astype(jnp.int32), meta)
        turn = (off - start).astype(jnp.int32) & (LANES - 1)
        meta = jnp.where(lane == devices + o, turn, meta)
        start = start + total
        last = (off + total)[chunks - 1 : chunks, :]
        out_ref[o, 4 * tiles : 4 * tiles + 8, :] = jnp.broadcast_to(last, (8, LANES))
    rank_ref[...] = rank.astype(jnp.int32)
    pos_ref[...] = pos.astype(jnp.int32)
    meta_ref[...] = meta
    copy = pltpu.make_async_copy(meta_ref, meta_s, sem)
    copy.start()

    def sort_chunk(c):
        hot = (iota((LANES, LANES), 0) == pos_ref[pl.ds(c, 1), :]).astype(jnp.float32).astype(jnp.bfloat16)
        items = iota((8, LANES), 1).astype(jnp.float32).astype(jnp.bfloat16)
        inverse = lax.dot_general(
            items, hot, (((1,), (1,)), ((), ())), preferred_element_type=jnp.float32
        ).astype(jnp.int32)
        data_ref[c] = jnp.take_along_axis(data_ref[c], inverse, axis=1, mode="promise_in_bounds")

    for c in range(chunks):
        sort_chunk(c)
    copy.wait()
    sub8 = iota((8, LANES), 0)
    lane8 = iota((8, LANES), 1)

    def place_chunk(c, carry):
        row = data_ref[c]

        def place(o):
            off = meta_s[c, o]
            where_to = pl.ds(4 * (off >> 7), 8)
            turned = pltpu.roll(row, meta_s[c, devices + o], 1)
            keep = (sub8 < 4) & (lane8 < (off & (LANES - 1)))
            out_ref[o, where_to, :] = jnp.where(keep, out_ref[o, where_to, :], turned)

        each(devices, place, 8)
        return carry

    counts = [out_ref[o, 4 * tiles : 4 * tiles + 8, :] for o in range(devices)] if devices <= 8 else None
    if counts is None:
        last_off = meta_ref
    lax.fori_loop(0, chunks, place_chunk, 0)
    for o in range(devices):
        if counts is not None:
            out_ref[o, 4 * tiles : 4 * tiles + 8, :] = counts[o]
        else:
            n = meta_s[chunks - 1, o] + jnp.sum((own_ref[chunks - 1 : chunks, :] == o).astype(jnp.int32))
            out_ref[o, 4 * tiles : 4 * tiles + 8, :] = jnp.full((8, LANES), n, jnp.int32).astype(jnp.float32)


def lookup_kernel(
    devices, tiles, field_ref, in_ref, out_ref, table, index_v, index_s, rows_ref, sem
):
    span = tiles + 1
    for s in range(devices):
        codes = in_ref[s, pl.ds(0, span, stride=4), :].astype(jnp.int32)
        is_count = iota((span, LANES), 0) == tiles
        index_v[pl.ds(s * span, span), :] = jnp.where(is_count, codes, codes >> 6)
    copy = pltpu.make_async_copy(index_v, index_s, sem)
    copy.start()

    def build(g, carry):
        block = field_ref[pl.ds(pl.multiple_of(g * 16, 16), 16), :].astype(jnp.float32)
        for x in range(7):
            table[pl.ds(g * 128 + x, 16, stride=8), :] = block[:, 64 * x : 64 * x + 128]
        return carry

    lax.fori_loop(0, field_ref.shape[0] // 16, build, 0)
    copy.wait()
    sub8 = iota((8, LANES), 0)

    def source(s):
        count = index_s[s * span + tiles, 0]

        def tile(t, carry):
            line = s * span + t
            for p in range(LANES):
                rows_ref[p : p + 1, :] = table[pl.ds(index_s[line, p], 1), :]
            cells = rows_ref[...].T
            query = in_ref[s, pl.ds(4 * t, 4), :]
            code = query[0:1].astype(jnp.int32)
            cy = jnp.broadcast_to((code >> 3) & 7, (8, LANES))
            cz = jnp.broadcast_to(code & 7, (8, LANES))
            fx = jnp.broadcast_to(query[1:2], (8, LANES))
            fy = jnp.broadcast_to(query[2:3], (8, LANES))
            fz = jnp.broadcast_to(query[3:4], (8, LANES))
            zero = jnp.zeros((8, LANES), jnp.float32)
            inter = [zero, zero]
            slope = [zero, zero]
            for y in range(8):
                low, high = cy == y, cy == y - 1
                weight = jnp.where(low, 1.0 - fy, jnp.where(high, fy, 0.0))
                sign = jnp.where(low, -1.0, jnp.where(high, 1.0, 0.0))
                for a in range(2):
                    v = cells[64 * a + 8 * y : 64 * a + 8 * y + 8, :]
                    inter[a] = inter[a] + weight * v
                    slope[a] = slope[a] + sign * v
            low, high = cz == sub8, cz == sub8 - 1
            weight = jnp.where(low, 1.0 - fz, jnp.where(high, fz, 0.0))
            sign = jnp.where(low, -1.0, jnp.where(high, 1.0, 0.0))
            mixed = (1.0 - fx) * inter[0] + fx * inter[1]
            parts = [
                weight * mixed,
                weight * (inter[1] - inter[0]),
                weight * ((1.0 - fx) * slope[0] + fx * slope[1]),
                sign * mixed,
            ]
            out_ref[s, pl.ds(4 * t, 4), :] = jnp.concatenate(
                [jnp.sum(q, axis=0, keepdims=True) for q in parts], axis=0
            )
            return carry

        lax.fori_loop(0, (count + LANES - 1) >> 7, tile, 0)

    lax.fori_loop(0, devices, lambda s, z: (source(s), z)[1], 0)


def greet(peers):
    barrier = pltpu.get_barrier_semaphore()
    for peer in peers:
        pl.semaphore_signal(barrier, inc=1, device_id=peer, device_id_type=MESH)
    pl.semaphore_wait(barrier, len(peers))


def peer_along(axis, size, step):
    return {axis: lax.rem(lax.axis_index(axis) + step, size)}


def starts(devices, lines, src_ref, dst_of, send_sem, recv_sem):
    me = lax.axis_index("map")
    copies = []
    for k in range(1, devices):
        to = lax.rem(me + k, devices)
        copy = pltpu.make_async_remote_copy(
            src_ref=src_ref.at[to, pl.ds(0, lines)],
            dst_ref=dst_of(k),
            send_sem=send_sem.at[k],
            recv_sem=recv_sem.at[k],
            device_id={"map": to},
            device_id_type=MESH,
        )
        copy.start()
        copies.append(copy)
    own = pltpu.make_async_copy(
        src_ref.at[me, pl.ds(0, lines)], dst_of(0), recv_sem.at[0]
    )
    own.start()
    return own, copies


def exchange_kernel(devices, lines, in_ref, out_ref, send_sem, recv_sem):
    greet([peer_along("map", devices, k) for k in range(1, devices)])
    me = lax.axis_index("map")
    own, copies = starts(
        devices, lines, in_ref, lambda k: out_ref.at[me, pl.ds(0, lines)], send_sem, recv_sem
    )
    own.wait()
    for copy in copies:
        copy.wait()


def combine_kernel(
    devices, reps, lines, in_ref, own_ref, rank_ref, meta_s, cost_ref, grad_ref,
    held, costs, send_sem, recv_sem, cost_send, cost_recv, *landed,
):
    greet(
        [peer_along("map", devices, k) for k in range(1, devices)]
        + [peer_along("rep", reps, k) for k in range(1, reps)]
    )
    own_copy, copies = starts(
        devices, lines, in_ref, lambda k: landed[k].at[pl.ds(0, lines)], send_sem, recv_sem
    )
    me = lax.axis_index("map")
    chunks = own_ref.shape[0]
    sub8 = iota((8, LANES), 0)
    half = (sub8 >= 4).astype(jnp.int32)
    for k in range(devices):
        if k == 0:
            own_copy.wait()
            source = me
        else:
            copies[k - 1].wait_recv()
            source = lax.rem(me + devices - k, devices)

        def chunk(c, carry):
            owner = jnp.broadcast_to(own_ref[pl.ds(c, 1), :], (8, LANES))
            rank = jnp.broadcast_to(rank_ref[pl.ds(c, 1), :], (8, LANES))
            which = (rank >> 7) - half
            w = meta_s[c, source] >> 7
            picked = jnp.take_along_axis(
                landed[k][pl.ds(4 * w, 8), :], rank & (LANES - 1), axis=1,
                mode="promise_in_bounds",
            )
            before = held[c] if k else jnp.zeros((8, LANES), jnp.float32)
            held[c] = jnp.where((owner == source) & (which == w), picked, before)
            return carry

        lax.fori_loop(0, chunks, chunk, 0, unroll=8)
    dist = held[:, 0, :] + held[:, 4, :]
    hinge = jnp.maximum(margin - dist, 0.0)
    halves = grad_ref.shape[2] // LANES
    quarter = chunks // halves
    rep = lax.axis_index("rep")
    for h in range(halves):
        here = hinge[h * quarter : (h + 1) * quarter]
        costs[0, :, h * LANES : (h + 1) * LANES] = jnp.sum(here * here, axis=0, keepdims=True)
    for n in range(3):
        grad = -2.0 * hinge * (held[:, 1 + n, :] + held[:, 5 + n, :])
        for h in range(halves):
            grad_ref[n, :, h * LANES : (h + 1) * LANES] = grad[h * quarter : (h + 1) * quarter]
    sums = []
    for k in range(1, reps):
        copy = pltpu.make_async_remote_copy(
            src_ref=costs.at[0],
            dst_ref=costs.at[k],
            send_sem=cost_send.at[k],
            recv_sem=cost_recv.at[k],
            device_id=peer_along("rep", reps, k),
            device_id_type=MESH,
        )
        copy.start()
        sums.append(copy)
    for copy in copies:
        copy.wait_send()
    total = costs[0]
    for k, copy in enumerate(sums):
        copy.wait()
        total = total + costs[k + 1]
    cost_ref[...] = total


def per_device(field_bricks, owners, bricks, corners, fraction):
    devices = lax.axis_size("map")
    trajectories_here, quarter = owners.shape
    row_count = trajectories_here * quarter
    capacity = 4 * row_count // devices
    tiles = -(-capacity // LANES)
    chunks = row_count // LANES
    lines = -(-(4 * tiles + 8) // 8) * 8
    buffer = jax.ShapeDtypeStruct((devices, lines, LANES), jnp.float32)
    flat = jax.ShapeDtypeStruct((chunks, LANES), jnp.int32)
    vm = pl.BlockSpec(memory_space=VMEM)
    sm = pl.BlockSpec(memory_space=SMEM)
    outgoing, own, rank, meta = pl.pallas_call(
        functools.partial(dispatch_kernel, devices, tiles),
        out_shape=(buffer, flat, flat, flat),
        in_specs=[vm] * 4,
        out_specs=(vm,) * 4,
        scratch_shapes=[
            VMEM((chunks, 8, LANES), jnp.float32),
            VMEM((chunks, LANES), jnp.int32),
            SMEM((chunks, LANES), jnp.int32),
            pltpu.SemaphoreType.DMA(()),
        ],
        name="dispatch",
    )(owners.T, bricks.T, corners.T, fraction.transpose(0, 2, 1))
    span = tiles + 1
    sems = pltpu.SemaphoreType.DMA((devices,))
    incoming = pl.pallas_call(
        functools.partial(exchange_kernel, devices, 4 * span),
        out_shape=buffer,
        in_specs=[vm],
        out_specs=vm,
        scratch_shapes=[sems, sems],
        compiler_params=pltpu.CompilerParams(collective_id=0, has_side_effects=True),
        name="send_queries",
    )(outgoing)
    located = pl.pallas_call(
        functools.partial(lookup_kernel, devices, tiles),
        out_shape=buffer,
        in_specs=[vm] * 2,
        out_specs=vm,
        scratch_shapes=[
            VMEM((field_bricks.shape[0] * 8, LANES), jnp.float32),
            VMEM((devices * span, LANES), jnp.int32),
            SMEM((devices * span, LANES), jnp.int32),
            VMEM((LANES, LANES), jnp.float32),
            pltpu.SemaphoreType.DMA(()),
        ],
        name="lookup",
    )(field_bricks, incoming)
    reps = lax.axis_size("rep")
    rep_sems = pltpu.SemaphoreType.DMA((reps,))
    cost, waypoint_grad = pl.pallas_call(
        functools.partial(combine_kernel, devices, reps, 4 * tiles),
        out_shape=(
            jax.ShapeDtypeStruct((1, trajectories_here), jnp.float32),
            jax.ShapeDtypeStruct((3, quarter, trajectories_here), jnp.float32),
        ),
        in_specs=[vm, vm, vm, sm],
        out_specs=(vm, vm),
        scratch_shapes=[
            VMEM((chunks, 8, LANES), jnp.float32),
            VMEM((reps, 1, trajectories_here), jnp.float32),
            sems, sems, rep_sems, rep_sems,
        ]
        + [VMEM((lines, LANES), jnp.float32)] * devices,
        compiler_params=pltpu.CompilerParams(collective_id=1, has_side_effects=True),
        name="combine",
    )(located, own, rank, meta)
    return cost.reshape(trajectories_here), waypoint_grad.transpose(0, 2, 1)


def solution(mesh):
    placed = (
        P("map", None),
        P("map", "rep"),
        P("map", "rep"),
        P("map", "rep"),
        P(None, "map", "rep"),
    )
    return jax.shard_map(
        per_device,
        mesh=mesh,
        in_specs=placed,
        out_specs=(P("map"), P(None, "map", "rep")),
        check_vma=False,
    )
```

profile of v0, /device:TPU:0, one launch (start us, length us, event | category | flops | bytes accessed | tf_op | source)
XLA Modules:
  0.0 63.9 jit_solution(11043439055163921765)
XLA Ops:
  0.6 6.5 %dispatch.1 = (f32[8,72,128]{2,1,0:T(8,128)}, s32[32,128]{1,0:T(8,128)}, s32[32,128]{1,0:T(8,128)}, s32[32,128]{1,0:T(8,128)}) custom-call(s32[16,256]{1,0:T(8,128)} %bitcast.8, s32[16,256]{1,0:T(8,128)} %bitcast.9, s32[16,256]{1,0:T(8,128)} %bitcast.10, f32[3,16,256]{2,1,0:T(8,128)} %bitcast.6), custom_call_target="tpu_custom_call" | custom-call | tf_op jit(solution)/shard_map/dispatch/pallas_call | solution.py:319
  7.1 12.6 %send_queries.1.in_ref = f32[8,72,128]{2,1,0:T(8,128)} custom-call(f32[8,72,128]{2,1,0:T(8,128)} %get-tuple-element.8.in_ref), custom_call_target="tpu_custom_call" | custom-call | tf_op jit(solution)/shard_map/send_queries/pallas_call | solution.py:334
  19.8 21.0 %lookup.1.in_ref = f32[8,72,128]{2,1,0:T(8,128)} custom-call(bf16[2048,512]{1,0:T(8,128)(2,1)} %field_ref.1, f32[8,72,128]{2,1,0:T(8,128)} %send_queries.1.in_ref), custom_call_target="tpu_custom_call" | custom-call | tf_op jit(solution)/shard_map/lookup/pallas_call | solution.py:343
  40.8 20.5 %combine.1 = (f32[1,256]{1,0:T(1,128)}, f32[3,16,256]{2,1,0:T(8,128)}) custom-call(f32[8,72,128]{2,1,0:T(8,128)} %lookup.1.in_ref, s32[32,128]{1,0:T(8,128)} %get-tuple-element.9.own_ref, s32[32,128]{1,0:T(8,128)} %get-tuple-element.10.rank_ref, s32[32,128]{1,0:T(8,128)} %get-tuple-element.11.meta_s), custom_call_target="tpu_custom_call" | custom-call | tf_op jit(solution)/shard_map/combine/pallas_call | solution.py:359
  61.3 1.2 %copy.9 = f32[256]{0:T(256)} copy(f32[256]{0:T(256)} %bitcast.11) | data formatting | bytes 2048
  62.5 1.4 %copy.10 = f32[3,256,16]{1,2,0:T(8,128)} copy(f32[3,256,16]{1,2,0:T(8,128)} %bitcast.7) | data formatting | bytes 98304
where the time goes:
time: 63.6 us; the launch traced here: 63.9 us
  Pallas kernels  60.6 us (95%)
  local copies, waits for them, and re-layouts  2.62 us (4%)
  between operations  0.66 us (1%)
    pallas_call x1, Pallas kernels, per_device(): pl.pallas_call(functools.partial(lookup_kernel, devices, tiles), out_shap...  21 us
    pallas_call x1, Pallas kernels, per_device(): pl.pallas_call(functools.partial(combine_kernel, devices, reps, 4 * tiles...  20.5 us
    pallas_call x1, Pallas kernels, per_device(): pl.pallas_call(functools.partial(exchange_kernel, devices, 4 * span), out...  12.6 us
    pallas_call x1, Pallas kernels, per_device(): pl.pallas_call(functools.partial(dispatch_kernel, devices, tiles), out_sh...  6.47 us
    unnamed x2, local copies, waits for them, and re-layouts  2.62 us

commit v1 on v0

--- a/solution.py
+++ b/solution.py
@@ -124,7 +124,7 @@
 
 
 def lookup_kernel(
-    devices, tiles, field_ref, in_ref, out_ref, table, index_v, index_s, rows_ref, sem
+    devices, tiles, table, in_ref, out_ref, index_v, index_s, rows_ref, sem
 ):
     span = tiles + 1
     for s in range(devices):
@@ -134,13 +134,6 @@
     copy = pltpu.make_async_copy(index_v, index_s, sem)
     copy.start()
 
-    def build(g, carry):
-        block = field_ref[pl.ds(pl.multiple_of(g * 16, 16), 16), :].astype(jnp.float32)
-        for x in range(7):
-            table[pl.ds(g * 128 + x, 16, stride=8), :] = block[:, 64 * x : 64 * x + 128]
-        return carry
-
-    lax.fori_loop(0, field_ref.shape[0] // 16, build, 0)
     copy.wait()
     sub8 = iota((8, LANES), 0)
 
@@ -223,12 +216,19 @@
     return own, copies
 
 
-def exchange_kernel(devices, lines, in_ref, out_ref, send_sem, recv_sem):
+def exchange_kernel(devices, lines, in_ref, field_ref, out_ref, table, send_sem, recv_sem):
     greet([peer_along("map", devices, k) for k in range(1, devices)])
     me = lax.axis_index("map")
     own, copies = starts(
         devices, lines, in_ref, lambda k: out_ref.at[me, pl.ds(0, lines)], send_sem, recv_sem
     )
+    def build(g, carry):
+        block = field_ref[pl.ds(pl.multiple_of(g * 16, 16), 16), :].astype(jnp.float32)
+        for x in range(7):
+            table[pl.ds(g * 128 + x, 16, stride=8), :] = block[:, 64 * x : 64 * x + 128]
+        return carry
+
+    lax.fori_loop(0, field_ref.shape[0] // 16, build, 0)
     own.wait()
     for copy in copies:
         copy.wait()
@@ -327,33 +327,35 @@
             SMEM((chunks, LANES), jnp.int32),
             pltpu.SemaphoreType.DMA(()),
         ],
+        compiler_params=pltpu.CompilerParams(vmem_limit_bytes=16 << 20),
         name="dispatch",
     )(owners.T, bricks.T, corners.T, fraction.transpose(0, 2, 1))
     span = tiles + 1
     sems = pltpu.SemaphoreType.DMA((devices,))
-    incoming = pl.pallas_call(
+    table = VMEM((field_bricks.shape[0] * 8, LANES), jnp.float32)
+    incoming, table = pl.pallas_call(
         functools.partial(exchange_kernel, devices, 4 * span),
-        out_shape=buffer,
-        in_specs=[vm],
-        out_specs=vm,
+        out_shape=(buffer, table),
+        in_specs=[vm, vm],
+        out_specs=(vm, vm),
         scratch_shapes=[sems, sems],
-        compiler_params=pltpu.CompilerParams(collective_id=0, has_side_effects=True),
+        compiler_params=pltpu.CompilerParams(collective_id=0, has_side_effects=True, vmem_limit_bytes=16 << 20),
         name="send_queries",
-    )(outgoing)
+    )(outgoing, field_bricks)
     located = pl.pallas_call(
         functools.partial(lookup_kernel, devices, tiles),
         out_shape=buffer,
         in_specs=[vm] * 2,
         out_specs=vm,
         scratch_shapes=[
-            VMEM((field_bricks.shape[0] * 8, LANES), jnp.float32),
             VMEM((devices * span, LANES), jnp.int32),
             SMEM((devices * span, LANES), jnp.int32),
             VMEM((LANES, LANES), jnp.float32),
             pltpu.SemaphoreType.DMA(()),
         ],
+        compiler_params=pltpu.CompilerParams(vmem_limit_bytes=16 << 20),
         name="lookup",
-    )(field_bricks, incoming)
+    )(table, incoming)
     reps = lax.axis_size("rep")
     rep_sems = pltpu.SemaphoreType.DMA((reps,))
     cost, waypoint_grad = pl.pallas_call(
@@ -370,7 +372,7 @@
             sems, sems, rep_sems, rep_sems,
         ]
         + [VMEM((lines, LANES), jnp.float32)] * devices,
-        compiler_params=pltpu.CompilerParams(collective_id=1, has_side_effects=True),
+        compiler_params=pltpu.CompilerParams(collective_id=1, has_side_effects=True, vmem_limit_bytes=16 << 20),
         name="combine",
     )(located, own, rank, meta)
     return cost.reshape(trajectories_here), waypoint_grad.transpose(0, 2, 1)

time: 63.6 us -> 54.8 us (0.86)
  Pallas kernels: 60.6 us -> 48.4 us
  local copies, waits for them, and re-layouts: 2.62 us -> 5.71 us
    pallas_call x1, Pallas kernels: 21 us -> 6.43 us  [per_device(): pl.pallas_call(functools.partial(lookup_kernel, devices, tiles), out_shap...]
    pallas_call x1, Pallas kernels: 12.6 us -> 16 us  [per_device(): pl.pallas_call(functools.partial(exchange_kernel, devices, 4 * span), out...]
    unnamed x2 -> x12, local copies, waits for them, and re-layouts: 2.62 us -> 5.71 us
    pallas_call x1, Pallas kernels: 6.47 us -> 4.97 us  [per_device(): pl.pallas_call(functools.partial(dispatch_kernel, devices, tiles), out_sh...]
where the time goes in v1:
time: 54.8 us
  Pallas kernels  48.4 us (88%)
  local copies, waits for them, and re-layouts  5.71 us (10%)
  between operations  0.68 us (1%)
    pallas_call x1, Pallas kernels, per_device(): pl.pallas_call(functools.partial(combine_kernel, devices, reps, 4 * tiles...  21 us
    pallas_call x1, Pallas kernels, per_device(): pl.pallas_call(functools.partial(exchange_kernel, devices, 4 * span), out...  16 us
    pallas_call x1, Pallas kernels, per_device(): pl.pallas_call(functools.partial(lookup_kernel, devices, tiles), out_shap...  6.43 us
    unnamed x12, local copies, waits for them, and re-layouts  5.71 us
    pallas_call x1, Pallas kernels, per_device(): pl.pallas_call(functools.partial(dispatch_kernel, devices, tiles), out_sh...  4.97 us

profile of v1, /device:TPU:0, one launch (start us, length us, event | category | flops | bytes accessed | tf_op | source)
XLA Modules:
  0.0 54.8 jit_solution(8213206592972754684)
XLA Ops:
  0.6 0.0 copy-start.1
  0.6 0.8 %copy-done.1 = f32[3,256,16]{1,2,0:T(8,128)S(1)} copy-done((f32[3,256,16]{1,2,0:T(8,128)S(1)}, f32[3,256,16]{1,2,0:T(8,128)}, u32[]{:S(2)}) %copy-start.1) | copy-done | bytes 49176
  1.4 0.0 copy-start.2
  1.4 0.7 %copy-done.2 = s32[256,16]{0,1:T(8,128)S(1)} copy-done((s32[256,16]{0,1:T(8,128)S(1)}, s32[256,16]{0,1:T(8,128)}, u32[]{:S(2)}) %copy-start.2) | copy-done | bytes 16408
  2.1 0.0 copy-start.3
  2.2 0.7 %copy-done.3 = s32[256,16]{0,1:T(8,128)S(1)} copy-done((s32[256,16]{0,1:T(8,128)S(1)}, s32[256,16]{0,1:T(8,128)}, u32[]{:S(2)}) %copy-start.3) | copy-done | bytes 16408
  2.9 0.0 copy-start.4
  2.9 0.7 %copy-done.4 = s32[256,16]{0,1:T(8,128)S(1)} copy-done((s32[256,16]{0,1:T(8,128)S(1)}, s32[256,16]{0,1:T(8,128)}, u32[]{:S(2)}) %copy-start.4) | copy-done | bytes 16408
  3.6 5.0 %dispatch.1 = (f32[8,72,128]{2,1,0:T(8,128)S(1)}, s32[32,128]{1,0:T(8,128)S(1)}, s32[32,128]{1,0:T(8,128)S(1)}, s32[32,128]{1,0:T(8,128)S(1)}) custom-call(s32[16,256]{1,0:T(8,128)S(1)} %bitcast.8, s32[16,256]{1,0:T(8,128)S(1)} %bitcast.9, s32[16,256]{1,0:T(8,128)S(1)} %bitcast.10, f32[3,16,256]{2,1,0:T(8,128)S(1)} %bitcast.6), custom_call_target="tpu_custom_call" | custom-call | tf_op jit(solution)/shard_map/dispatch/pallas_call | solution.py:319
  8.6 0.0 copy-start
  8.6 1.6 %copy-done = bf16[2048,512]{1,0:T(8,128)(2,1)S(1)} copy-done((bf16[2048,512]{1,0:T(8,128)(2,1)S(1)}, bf16[2048,512]{1,0:T(8,128)(2,1)}, u32[]{:S(2)}) %copy-start) | copy-done | bytes 2097176
  10.2 16.0 %send_queries.1 = (f32[8,72,128]{2,1,0:T(8,128)S(1)}, f32[16384,128]{1,0:T(8,128)S(1)}) custom-call(f32[8,72,128]{2,1,0:T(8,128)S(1)} %get-tuple-element.10.in_ref, bf16[2048,512]{1,0:T(8,128)(2,1)S(1)} %copy-done), custom_call_target="tpu_custom_call" | custom-call | tf_op jit(solution)/shard_map/send_queries/pallas_call | solution.py:336
  26.2 6.4 %lookup.1.in_ref = f32[8,72,128]{2,1,0:T(8,128)S(1)} custom-call(f32[16384,128]{1,0:T(8,128)S(1)} %get-tuple-element.11.table, f32[8,72,128]{2,1,0:T(8,128)S(1)} %get-tuple-element.12.in_ref), custom_call_target="tpu_custom_call" | custom-call | tf_op jit(solution)/shard_map/lookup/pallas_call | solution.py:345
  32.6 21.0 %combine.1 = (f32[1,256]{1,0:T(1,128)S(1)}, f32[3,16,256]{2,1,0:T(8,128)S(1)}) custom-call(f32[8,72,128]{2,1,0:T(8,128)S(1)} %lookup.1.in_ref, s32[32,128]{1,0:T(8,128)S(1)} %get-tuple-element.13.own_ref, s32[32,128]{1,0:T(8,128)S(1)} %get-tuple-element.14.rank_ref, s32[32,128]{1,0:T(8,128)S(1)} %get-tuple-element.15.meta_s), custom_call_target="tpu_custom_call" | custom-call | tf_op jit(solution)/shard_map/combine/pallas_call | solution.py:361
  53.6 0.6 %copy.9 = f32[256]{0:T(256)} copy(f32[256]{0:T(256)S(1)} %bitcast.11) | data formatting | bytes 2048
  54.2 0.6 %copy.10 = f32[3,256,16]{1,2,0:T(8,128)} copy(f32[3,256,16]{1,2,0:T(8,128)S(1)} %bitcast.7) | data formatting | bytes 98304
Async XLA Ops:
  0.6 0.8 %copy-start.1 = (f32[3,256,16]{1,2,0:T(8,128)S(1)}, f32[3,256,16]{1,2,0:T(8,128)}, u32[]{:S(2)}) copy-start(f32[3,256,16]{1,2,0:T(8,128)} %param.9) | copy-start | bytes 147460
  1.4 0.7 %copy-start.2 = (s32[256,16]{0,1:T(8,128)S(1)}, s32[256,16]{0,1:T(8,128)}, u32[]{:S(2)}) copy-start(s32[256,16]{0,1:T(8,128)} %param.6) | copy-start | bytes 49156
  2.1 0.7 %copy-start.3 = (s32[256,16]{0,1:T(8,128)S(1)}, s32[256,16]{0,1:T(8,128)}, u32[]{:S(2)}) copy-start(s32[256,16]{0,1:T(8,128)} %param.7) | copy-start | bytes 49156
  2.9 0.7 %copy-start.4 = (s32[256,16]{0,1:T(8,128)S(1)}, s32[256,16]{0,1:T(8,128)}, u32[]{:S(2)}) copy-start(s32[256,16]{0,1:T(8,128)} %param.8) | copy-start | bytes 49156
  8.6 1.6 %copy-start = (bf16[2048,512]{1,0:T(8,128)(2,1)S(1)}, bf16[2048,512]{1,0:T(8,128)(2,1)}, u32[]{:S(2)}) copy-start(bf16[2048,512]{1,0:T(8,128)(2,1)} %field_ref.1) | copy-start | bytes 6291460
